TPU v7x, 256 devices: a whole 4x4x8 slice. The times are simulated.
256 devices in a mesh: toa: 128 (over z, y, x), rep: 2 (over core).
Axes of the slice: x: 4, y: 4, z: 8, core: 2. Of those that a mesh axis runs over, the one named last changes fastest.
Arguments:
- residual: float32 [16384, 256], P('toa'), may hold values from -6 to 6
- toa_error: float32 [16384, 256], P('toa'), may hold values from 0.3 to 3
- basis_rows: bfloat16 [16384, 100, 256], P('toa', 'rep'), may hold values from -0.041432038 to 0.041432038
- efac_table: float32 [128, 64], replicated, may hold values from 0.5 to 2
- equad_table: float32 [128, 64], replicated, may hold values from 0.1 to 1
- pulsar: int32 [16384], P('toa'), may hold values from 0 to 127
- backend: int32 [16384], P('toa'), may hold values from 0 to 63
- counts: int32 [16384], P('toa'), may hold values from 64 to 256
- owner_slot: int32 [16384], P('toa'), may hold values from 0 to 16383, as said below
Outputs:
- gram_matrix: float32 [128, 100, 100], P('toa', None, 'rep')
- projection: float32 [128, 100], P('toa', 'rep')
- whitened: float32 [16384, 256], P('toa')
Inputs may be any that keep to these rules, and one draw needn't show every extreme that they name: A permutation of the 16384 slots, independent of pulsar and backend; owner_slot // 128 is the device index along toa that holds the tile's output row and owner_slot % 128 its place there; each device's tiles go exactly 1 to each device.
All inputs are finite; a program needn't handle non-finite values.
Results may differ from a plain program's by a relative error of at most 0.0032.
Values may be sent and summed in bfloat16 or wider, within the bound.
No kernel may reach another device: no remote copies, remote signals or barrier semaphores. Data moves between devices by JAX's collectives and lax.ppermute only.
A program may use at most 64 MiB of HBM per device.

v0:
```python
import jax
import jax.numpy as jnp
from jax import lax
from jax.sharding import Mesh
from jax.sharding import PartitionSpec as P

TOA = ("toa_0", "toa_1", "toa_2")


def in_blocks(value, dim, peers):
    shape = value.shape
    pieces = value.reshape(*shape[:dim], peers, shape[dim] // peers, *shape[dim + 1 :])
    return jnp.moveaxis(pieces, dim, 0)


def sum_at_owner(value, axis, dim):
    peers = lax.axis_size(axis)
    pieces = lax.all_to_all(in_blocks(value, dim, peers), axis, 0, 0, tiled=True)
    return jnp.sum(pieces, axis=0)


def summed_rows(value, axes, dim):
    far, near = axes
    own = sum_at_owner(in_blocks(value, dim, lax.axis_size(far)), near, dim + 1)
    return jnp.sum(lax.all_to_all(own, far, 0, 0, tiled=True), axis=0)


def side_by_side(arrays, axis, dim, along):
    columns = [a.reshape(*a.shape[:along], -1) for a in arrays]
    both = jnp.concatenate(columns, axis=along)
    filled, at, done = (summed_rows(both, axis, dim), 0, [])
    for a, column in zip(arrays, columns):
        section = filled[..., at : at + column.shape[along]]
        done.append(section.reshape(*section.shape[:along], *a.shape[along:]))
        at += column.shape[along]
    return tuple(done)


def sent_together(arrays, axis, split_dim, concat_dim, along):
    ends, at = ([], 0)
    for a in arrays[:-1]:
        at += a.shape[along]
        ends.append(at)
    both = jnp.concatenate(arrays, axis=along)
    return tuple(
        jnp.split(
            lax.all_to_all(both, axis, split_axis=split_dim, concat_axis=concat_dim, tiled=True),
            ends,
            axis=along,
        )
    )


def lookup(small_table, onehot_pulsar, onehot_backend):
    table_rows = jnp.dot(onehot_pulsar, small_table, precision=lax.Precision.HIGHEST)
    return jnp.sum(table_rows * onehot_backend, axis=1)


def tile_weights(residual, toa_error, pulsar, backend, counts, efac_table, equad_table):
    onehot_pulsar = (
        pulsar[:, None] == jnp.arange(efac_table.shape[0], dtype=jnp.int32)[None, :]
    ).astype(jnp.float32)
    onehot_backend = (
        backend[:, None] == jnp.arange(efac_table.shape[1], dtype=jnp.int32)[None, :]
    ).astype(jnp.float32)
    factor = lookup(efac_table, onehot_pulsar, onehot_backend)
    floor_term = lookup(equad_table, onehot_pulsar, onehot_backend)
    valid_rows = jnp.arange(residual.shape[1], dtype=jnp.int32)[None, :] < counts[:, None]
    weight = jnp.where(
        valid_rows, 1.0 / (factor[:, None] ** 2 * toa_error**2 + floor_term[:, None] ** 2), 0.0
    )
    return (onehot_pulsar, weight)


def pulsar_terms(basis_own, weight, residual, onehot_pulsar):
    scaled = (weight[:, None, :] * basis_own).astype(jnp.bfloat16)
    weighted_res = (weight * residual).astype(jnp.bfloat16)
    tile_gram = jnp.einsum(
        "tkr,tjr->tkj",
        lax.all_gather(basis_own, "rep", axis=1, tiled=True),
        scaled,
        preferred_element_type=jnp.float32,
    )
    tile_proj = jnp.einsum(
        "tjr,tr->tj", basis_own, weighted_res, preferred_element_type=jnp.float32
    )
    tile_total, full_width, half_width = tile_gram.shape
    pulsar_total = onehot_pulsar.shape[1]
    gram_part = jnp.dot(
        onehot_pulsar.T,
        tile_gram.reshape(tile_total, full_width * half_width),
        precision=lax.Precision.HIGHEST,
    )
    gram_part = gram_part.reshape(pulsar_total, full_width, half_width)
    proj_part = jnp.dot(onehot_pulsar.T, tile_proj, precision=lax.Precision.HIGHEST)
    return side_by_side((gram_part, proj_part), ("toa_0", ("toa_1", "toa_2")), 0, 1)


def shards(
    residual, toa_error, basis_rows, efac_table, equad_table, pulsar, backend, counts, owner_slot
):
    tile_count = residual.shape[0]
    peer_count = lax.axis_size(TOA)
    per_peer = tile_count // peer_count
    owner_dev = owner_slot // tile_count
    owner_place = owner_slot % tile_count
    onehot_dest = (owner_dev[:, None] == jnp.arange(peer_count, dtype=jnp.int32)[None, :]).astype(
        jnp.int32
    )
    bucket_rank = jnp.sum((jnp.cumsum(onehot_dest, axis=0) - 1) * onehot_dest, axis=1)
    send_position = owner_dev * per_peer + bucket_rank
    send_order = (
        jnp.zeros((tile_count,), jnp.int32)
        .at[send_position]
        .set(jnp.arange(tile_count, dtype=jnp.int32))
    )
    onehot_pulsar, weight = tile_weights(
        residual, toa_error, pulsar, backend, counts, efac_table, equad_table
    )
    whitened_local = jnp.sqrt(weight) * residual
    place_float = owner_place[send_order][:, None].astype(jnp.float32)
    moved_white, moved_place = sent_together(
        (whitened_local[send_order], place_float), TOA, 0, 0, 1
    )
    whitened = jnp.zeros_like(moved_white).at[moved_place[:, 0].astype(jnp.int32)].set(moved_white)
    gram_matrix, projection = pulsar_terms(basis_rows, weight, residual, onehot_pulsar)
    return (gram_matrix, projection, whitened)


def solution(mesh):
    split = Mesh(
        mesh.devices.reshape(8, 4, 4, mesh.shape["rep"]), ("toa_0", "toa_1", "toa_2", "rep")
    )
    placed = (
        P(TOA, None),
        P(TOA, None),
        P(TOA, "rep", None),
        P(),
        P(),
        P(TOA),
        P(TOA),
        P(TOA),
        P(TOA),
    )
    return jax.shard_map(
        shards,
        mesh=split,
        in_specs=placed,
        out_specs=(P(TOA, None, "rep"), P(TOA, "rep"), P(TOA, None)),
        check_vma=False,
    )
```

profile of v0, /device:TPU:2, one launch (start us, length us, event | category | flops | bytes accessed | tf_op | source)
XLA Modules:
  0.0 154.6 jit_solution(5533874653531388217)
XLA Ops:
  7.3 0.7 all-gather.2.cloned.1.call-update
  8.0 0.3 fusion.10
  8.3 0.3 fusion.11
  8.6 1.6 %sqrt_multiply_fusion = (f32[128,256]{1,0:T(8,128)S(1)}, f32[128,256]{1,0:T(8,128)S(1)}) fusion(f32[128,256]{1,0:T(8,128)} %param.9, f32[128]{0:T(128)S(1)} %integer_pow.21, f32[128,256]{1,0:T(8,128)} %param.10, f32[128]{0:T(128)S(1)} %integer_pow.19, s32[128]{0:T(128)S(1)} %copy-done.3), kind=kLoop, calls=%fused_computation.21 | loop fusion | flops 229376 | bytes 525824 | tf_op jit(solution)/shard_map/mul | solution.py:120
  10.2 0.9 fusion.15
  11.2 1.9 %fusion.2 = f32[128,1,50]{2,1,0:T(1,128)S(1)} fusion(bf16[128,50,256]{2,0,1:T(8,128)(2,1)S(1)} %copy-done.1, bf16[128,256,1]{1,0,2:T(8,128)(2,1)S(1)} %fusion.15), kind=kOutput, calls=%fused_computation.7 | convolution fusion | flops 3276800 | bytes 3367936 | tf_op jit(solution)/shard_map/tjr,tr->tj/dot_general | solution.py:84
  13.1 0.3 fusion.18
  13.3 1.0 multiply_convert_fusion
  14.3 21.0 %all-gather.2.cloned.1.call-done = bf16[128,100,256]{2,0,1:T(8,128)(2,1)} async-done(((bf16[128,50,256]{2,0,1:T(8,128)(2,1)}), bf16[128,100,256]{2,0,1:T(8,128)(2,1)}) %all-gather.2.cloned.1.call-update) | async-done | bytes 6553616 | tf_op jit(solution)/shard_map/all_gather | solution.py:80
  35.3 10.3 %fusion.5 = f32[128,100,50]{1,2,0:T(8,128)} fusion(bf16[128,100,256]{2,0,1:T(8,128)(2,1)} %all-gather.2.cloned.1.call-done, bf16[128,50,256]{2,0,1:T(8,128)(2,1)S(1)} %multiply_convert_fusion), kind=kOutput, calls=%fused_computation.11 | convolution fusion | flops 327680000 | bytes 12390400 | tf_op jit(solution)/shard_map/tkr,tjr->tkj/dot_general | solution.py:78
  45.6 3.7 %copy.31 = f32[128,100,50]{0,2,1:T(8,128)S(1)} copy(f32[128,100,50]{1,2,0:T(8,128)} %fusion.5) | data formatting | bytes 5120000 | tf_op jit(solution)/shard_map/tkr,tjr->tkj/dot_general | solution.py:78
  49.3 1.7 %reshape.38 = f32[128,5000]{0,1:T(8,128)} reshape(f32[128,100,50]{0,2,1:T(8,128)S(1)} %copy.31) | data formatting | bytes 5120000 | tf_op jit(solution)/shard_map/reshape | solution.py:91
  50.9 4.0 %fusion.19 = f32[128,5000]{0,1:T(8,128)S(1)} fusion(f32[128,5000]{0,1:T(8,128)} %reshape.38, s32[128]{0:T(128)S(1)} %copy-done.4), kind=kOutput, calls=%fused_computation.32 | convolution fusion | flops 983056384 | bytes 5120512 | tf_op jit(solution)/shard_map/dot_general | solution.py:89
  54.9 1.7 %pad_maximum_fusion = f32[128,5050]{0,1:T(8,128)} fusion(f32[128,50]{0,1:T(8,128)S(1)} %fusion.18, f32[128,5000]{0,1:T(8,128)S(1)} %fusion.19), kind=kLoop, calls=%fused_computation.10 | loop fusion | flops 646400 | bytes 5171200 | tf_op jit(solution)/shard_map/concatenate | solution.py:30
  56.6 2.1 %copy.32 = f32[128,5050]{1,0:T(8,128)S(1)} copy(f32[128,5050]{0,1:T(8,128)} %pad_maximum_fusion) | data formatting | bytes 5171200 | tf_op jit(solution)/shard_map/concatenate | solution.py:30
  58.7 3.0 %copy.33 = f32[16,8,1,5050]{3,1,2,0:T(8,128)} copy(f32[16,8,1,5050]{3,0,1,2:T(8,128)S(1)} %bitcast.28) | data formatting | bytes 5171200 | tf_op jit(solution)/shard_map/transpose | solution.py:13
  61.8 7.4 %all-to-all-start = ((f32[16,8,1,5050]{3,1,2,0:T(8,128)}), f32[16,8,1,5050]{3,1,2,0:T(8,128)S(1)}, u32[]{:S(2)}, u32[]{:S(2)}) async-start(f32[16,8,1,5050]{3,1,2,0:T(8,128)} %copy.33), calls=%async_computation | async-start | bytes 5242880 | tf_op jit(solution)/shard_map/all_to_all | solution.py:18
  69.3 0.2 reduce_window_sum.11
  69.5 0.2 select_reduce_fusion
  69.7 1.0 scatter_custom_fusion
  70.7 1.2 gather_fusion.1
  72.0 0.8 gather_fusion
  72.8 0.9 copy.35
  73.7 32.2 %all-to-all-done = f32[16,8,1,5050]{3,1,2,0:T(8,128)S(1)} async-done(((f32[16,8,1,5050]{3,1,2,0:T(8,128)}), f32[16,8,1,5050]{3,1,2,0:T(8,128)S(1)}, u32[]{:S(2)}, u32[]{:S(2)}) %all-to-all-start) | async-done | bytes 2585632 | tf_op jit(solution)/shard_map/all_to_all | solution.py:18
  105.9 15.0 %all-to-all-start.2 = ((f32[128,1,257]{2,1,0:T(1,128)}), f32[128,1,257]{2,1,0:T(1,128)S(1)}, u32[]{:S(2)}, u32[]{:S(2)}) async-start(f32[128,1,257]{2,1,0:T(1,128)} %copy.35), calls=%async_computation.2 | async-start | bytes 393216 | tf_op jit(solution)/shard_map/all_to_all | solution.py:47
  121.0 0.8 reduce_sum.52
  121.8 11.6 %all-to-all-done.2 = f32[128,1,257]{2,1,0:T(1,128)S(1)} async-done(((f32[128,1,257]{2,1,0:T(1,128)}), f32[128,1,257]{2,1,0:T(1,128)S(1)}, u32[]{:S(2)}, u32[]{:S(2)}) %all-to-all-start.2) | async-done | bytes 131616 | tf_op jit(solution)/shard_map/all_to_all | solution.py:47
  133.4 3.4 %all-to-all-start.1 = ((f32[8,1,5050]{2,1,0:T(1,128)}), f32[8,1,5050]{2,1,0:T(1,128)S(1)}, u32[]{:S(2)}, u32[]{:S(2)}) async-start(f32[8,1,5050]{2,1,0:T(1,128)} %reduce_sum.52), calls=%async_computation.1 | async-start | bytes 327680 | tf_op jit(solution)/shard_map/all_to_all | solution.py:25
  137.0 1.6 %scatter_custom_fusion.1 = f32[128,256]{1,0:T(8,128)} fusion(s32[128]{0:T(128)S(1)} %fusion.24, f32[128,257]{1,0:T(8,128)S(1)} %bitcast.29, f32[]{:T(128)} %constant.37.clone.1), kind=kCustom, calls=%fused_computation.18 | custom fusion | bytes 262148 | tf_op jit(solution)/shard_map/scatter | solution.py:125
  138.6 7.6 %all-to-all-done.1 = f32[8,1,5050]{2,1,0:T(1,128)S(1)} async-done(((f32[8,1,5050]{2,1,0:T(1,128)}), f32[8,1,5050]{2,1,0:T(1,128)S(1)}, u32[]{:S(2)}, u32[]{:S(2)}) %all-to-all-start.1) | async-done | bytes 161632 | tf_op jit(solution)/shard_map/all_to_all | solution.py:25
  146.3 0.6 slice.13
  147.1 0.7 copy.38
  (35 shorter events, 0.9 us)
Async XLA Ops:
  7.2 0.8 copy-start
  7.2 4.0 %copy-start.1 = (bf16[128,50,256]{2,0,1:T(8,128)(2,1)S(1)}, bf16[128,50,256]{2,0,1:T(8,128)(2,1)}, u32[]{:S(2)}) copy-start(bf16[128,50,256]{2,0,1:T(8,128)(2,1)} %param.11) | copy-start | bytes 9830404
  7.2 0.8 copy-start.4
  7.2 0.8 copy-start.6
  7.2 1.1 copy-start.5
  7.2 1.4 copy-start.3
  7.2 28.1 %all-gather.2.cloned.1.call-start = ((), (), s32[]{:S(2)}) async-start(), calls=%async_computation.3 | async-start | bytes 9830400 | tf_op jit(solution)/shard_map/all_gather | solution.py:80
  8.0 5.3 %copy-start.2 = (bf16[128,50,256]{2,0,1:T(8,128)(2,1)S(1)}, bf16[128,50,256]{2,0,1:T(8,128)(2,1)}, u32[]{:S(2)}) copy-start(bf16[128,50,256]{2,0,1:T(8,128)(2,1)} %param.11) | copy-start | bytes 9830404
  61.8 7.4 %copy-start.7 = (s32[128]{0:T(128)S(1)}, s32[128]{0:T(128)}, u32[]{:S(2)}) copy-start(s32[128]{0:T(128)} %param.17) | copy-start | bytes 1540
  61.8 44.1 %all-to-all-start = ((f32[16,8,1,5050]{3,1,2,0:T(8,128)}), f32[16,8,1,5050]{3,1,2,0:T(8,128)S(1)}, u32[]{:S(2)}, u32[]{:S(2)}) async-start(f32[16,8,1,5050]{3,1,2,0:T(8,128)} %copy.33), calls=%async_computation | async-start | bytes 5242880 | tf_op jit(solution)/shard_map/all_to_all | solution.py:18
  105.9 27.5 %all-to-all-start.2 = ((f32[128,1,257]{2,1,0:T(1,128)}), f32[128,1,257]{2,1,0:T(1,128)S(1)}, u32[]{:S(2)}, u32[]{:S(2)}) async-start(f32[128,1,257]{2,1,0:T(1,128)} %copy.35), calls=%async_computation.2 | async-start | bytes 393216 | tf_op jit(solution)/shard_map/all_to_all | solution.py:47
  133.4 12.7 %all-to-all-start.1 = ((f32[8,1,5050]{2,1,0:T(1,128)}), f32[8,1,5050]{2,1,0:T(1,128)S(1)}, u32[]{:S(2)}, u32[]{:S(2)}) async-start(f32[8,1,5050]{2,1,0:T(1,128)} %reduce_sum.52), calls=%async_computation.1 | async-start | bytes 327680 | tf_op jit(solution)/shard_map/all_to_all | solution.py:25
Sparse Core Ops, SparseCore 0:
  9.8 25.4 all-gather.1
where the time goes:
time: 155 us
  waiting for transfers between devices  73.1 us (47%)
  starting transfers between devices  25.8 us (17%)
  local copies, waits for them, and re-layouts  18.5 us (12%)
  matrix products  17 us (11%)
  between operations  14.3 us (9%)
  other arithmetic  5.89 us (4%)
    all_to_all x1, waiting for transfers between devices, sum_at_owner(): lax.all_to_all(in_blocks(value, dim, peers), axis, 0, 0, tiled=True)  32.2 us
    all_gather x1, waiting for transfers between devices, pulsar_terms(): lax.all_gather(basis_own, 'rep', axis=1, tiled=True)  21 us
    all_to_all x1, starting transfers between devices, sent_together(): lax.all_to_all(both, axis, split_axis=split_dim, concat_axis=concat_dim,...  15 us
    all_to_all x1, waiting for transfers between devices, sent_together(): lax.all_to_all(both, axis, split_axis=split_dim, concat_axis=concat_dim,...  11.6 us
    dot_general x1, matrix products, pulsar_terms(): jnp.einsum('tkr,tjr->tkj', lax.all_gather(basis_own, 'rep', axis=1, tiled...  10.3 us
    all_to_all x1, waiting for transfers between devices, summed_rows(): return jnp.sum(lax.all_to_all(own, far, 0, 0, tiled=True), axis=0)  7.56 us
    all_to_all x1, starting transfers between devices, sum_at_owner(): lax.all_to_all(in_blocks(value, dim, peers), axis, 0, 0, tiled=True)  7.4 us
    dot_general x1, matrix products, pulsar_terms(): jnp.dot(onehot_pulsar.T, tile_gram.reshape(tile_total, full_width * half_...  4 us
  transfers between devices with their start and end apart: 4, of which 4 were waited for; matrix products, arithmetic and copies ran while one was open for 9% of the time, Pallas kernels for 0%

commit v1 on v0

--- a/solution.py
+++ b/solution.py
@@ -1,3 +1,4 @@
+import functools
 import jax
 import jax.numpy as jnp
 from jax import lax
@@ -5,6 +6,21 @@
 from jax.sharding import PartitionSpec as P
 
 TOA = ("toa_0", "toa_1", "toa_2")
+
+
+def pieces_all_end(v0, axis_id):
+    wide_n = jax.lax.axis_size(axis_id)
+    reply = jax.lax.all_to_all(
+        jnp.tile(v0, [wide_n if i == 1 else 1 for i in range(v0.ndim)]),
+        axis_id,
+        split_axis=1,
+        concat_axis=1,
+        tiled=True,
+    )
+    return reply
+
+
+pack_counts = functools.partial(pieces_all_end, axis_id="rep")
 
 
 def in_blocks(value, dim, peers):
@@ -76,10 +92,7 @@
     scaled = (weight[:, None, :] * basis_own).astype(jnp.bfloat16)
     weighted_res = (weight * residual).astype(jnp.bfloat16)
     tile_gram = jnp.einsum(
-        "tkr,tjr->tkj",
-        lax.all_gather(basis_own, "rep", axis=1, tiled=True),
-        scaled,
-        preferred_element_type=jnp.float32,
+        "tkr,tjr->tkj", pack_counts(basis_own), scaled, preferred_element_type=jnp.float32
     )
     tile_proj = jnp.einsum(
         "tjr,tr->tj", basis_own, weighted_res, preferred_element_type=jnp.float32

time: 155 us -> 133 us (0.86)
  waiting for transfers between devices: 73.1 us -> 51.5 us
  between operations: 14.3 us -> 0.95 us
  starting transfers between devices: 25.8 us -> 33.9 us
  local copies, waits for them, and re-layouts: 18.5 us -> 23.9 us
    all_gather x1 -> x0, waiting for transfers between devices: 21 us -> none  [pulsar_terms(): lax.all_gather(basis_own, 'rep', axis=1, tiled=True)]
    all_to_all x0 -> x1, starting transfers between devices: none -> 6.5 us  [pieces_all_end(): jax.lax.all_to_all(jnp.tile(v0, [wide_n if i == 1 else 1 for i in range(v...]
    another operation x0 -> x1, local copies, waits for them, and re-layouts: none -> 5.46 us  [pieces_all_end(): jnp.tile(v0, [wide_n if i == 1 else 1 for i in range(v0.ndim)])]
    convert_element_type x1, other arithmetic: 0.95 us -> 2.9 us  [pulsar_terms(): scaled = (weight[:, None, :] * basis_own).astype(jnp.bfloat16)]
  transfers between devices with their start and end apart: 4 -> 4, of which waited for: 4 -> 4; matrix products, arithmetic and copies ran while one was open for 9% -> 10% of each run, Pallas kernels for 0% -> 0%
where the time goes in v1:
time: 133 us
  waiting for transfers between devices  51.5 us (39%)
  starting transfers between devices  33.9 us (25%)
  local copies, waits for them, and re-layouts  23.9 us (18%)
  matrix products  17 us (13%)
  other arithmetic  5.46 us (4%)
    all_to_all x1, waiting for transfers between devices, sum_at_owner(): lax.all_to_all(in_blocks(value, dim, peers), axis, 0, 0, tiled=True)  32.1 us
    all_to_all x1, starting transfers between devices, sent_together(): lax.all_to_all(both, axis, split_axis=split_dim, concat_axis=concat_dim,...  16.4 us
    all_to_all x1, waiting for transfers between devices, sent_together(): lax.all_to_all(both, axis, split_axis=split_dim, concat_axis=concat_dim,...  11.6 us
    dot_general x1, matrix products, pulsar_terms(): jnp.einsum('tkr,tjr->tkj', pack_counts(basis_own), scaled, preferred_elem...  10.3 us
    all_to_all x1, starting transfers between devices, sum_at_owner(): lax.all_to_all(in_blocks(value, dim, peers), axis, 0, 0, tiled=True)  7.61 us
    all_to_all x1, waiting for transfers between devices, summed_rows(): return jnp.sum(lax.all_to_all(own, far, 0, 0, tiled=True), axis=0)  7.56 us
    all_to_all x1, starting transfers between devices, pieces_all_end(): jax.lax.all_to_all(jnp.tile(v0, [wide_n if i == 1 else 1 for i in range(v...  6.5 us
    another operation x1, local copies, waits for them, and re-layouts, pieces_all_end(): jnp.tile(v0, [wide_n if i == 1 else 1 for i in range(v0.ndim)])  5.46 us
  transfers between devices with their start and end apart: 4, of which 4 were waited for; matrix products, arithmetic and copies ran while one was open for 10% of the time, Pallas kernels for 0%

profile of v1, /device:TPU:2, one launch (start us, length us, event | category | flops | bytes accessed | tf_op | source)
XLA Modules:
  0.0 132.8 jit_solution(13534905810883557754)
XLA Ops:
  0.6 5.5 %tile.4 = bf16[128,2,50,256]{3,0,2,1:T(8,128)(2,1)} broadcast(bf16[128,50,256]{2,0,1:T(8,128)(2,1)} %param.11), dimensions={0,2,3} | broadcast | bytes 9830400 | tf_op jit(solution)/shard_map/tile | solution.py:14
  6.1 6.5 %all-to-all-start = ((bf16[128,100,256]{2,0,1:T(8,128)(2,1)}), bf16[128,100,256]{2,0,1:T(8,128)(2,1)}, u32[]{:S(2)}, u32[]{:S(2)}) async-start(bf16[128,100,256]{2,0,1:T(8,128)(2,1)} %bitcast.27), calls=%async_computation | async-start | bytes 13107200 | tf_op jit(solution)/shard_map/all_to_all | solution.py:13
  12.7 0.3 fusion.11
  13.0 0.3 fusion.10
  13.3 0.1 sqrt_multiply_fusion
  13.5 2.9 %multiply_convert_fusion = bf16[128,50,256]{2,0,1:T(8,128)(2,1)S(1)} fusion(bf16[128,50,256]{2,0,1:T(8,128)(2,1)} %param.11, f32[128,256]{1,0:T(8,128)S(1)} %get-tuple-element.13), kind=kLoop, calls=%fused_computation.6 | loop fusion | flops 4915200 | bytes 6684672 | tf_op jit(solution)/shard_map/convert_element_type | solution.py:92
  16.4 1.9 %fusion.2 = f32[128,1,50]{2,1,0:T(1,128)S(1)} fusion(bf16[128,50,256]{2,0,1:T(8,128)(2,1)S(1)} %copy-done.1, bf16[128,256,1]{1,0,2:T(8,128)(2,1)S(1)} %fusion.15), kind=kOutput, calls=%fused_computation.7 | convolution fusion | flops 3276800 | bytes 3367936 | tf_op jit(solution)/shard_map/tjr,tr->tj/dot_general | solution.py:97
  18.3 0.3 fusion.18
  18.6 0.3 all-to-all-done
  18.8 10.3 %fusion.5 = f32[128,100,50]{1,2,0:T(8,128)} fusion(bf16[128,100,256]{2,0,1:T(8,128)(2,1)} %all-to-all-done, bf16[128,50,256]{2,0,1:T(8,128)(2,1)S(1)} %multiply_convert_fusion), kind=kOutput, calls=%fused_computation.11 | convolution fusion | flops 327680000 | bytes 12390400 | tf_op jit(solution)/shard_map/tkr,tjr->tkj/dot_general | solution.py:94
  29.1 3.7 %copy.31 = f32[128,100,50]{0,2,1:T(8,128)S(1)} copy(f32[128,100,50]{1,2,0:T(8,128)} %fusion.5) | data formatting | bytes 5120000 | tf_op jit(solution)/shard_map/tkr,tjr->tkj/dot_general | solution.py:94
  32.8 1.7 %reshape.42 = f32[128,5000]{0,1:T(8,128)} reshape(f32[128,100,50]{0,2,1:T(8,128)S(1)} %copy.31) | data formatting | bytes 5120000 | tf_op jit(solution)/shard_map/reshape | solution.py:104
  34.4 4.0 %fusion.19 = f32[128,5000]{0,1:T(8,128)S(1)} fusion(f32[128,5000]{0,1:T(8,128)} %reshape.42, s32[128]{0:T(128)S(1)} %copy-done.5), kind=kOutput, calls=%fused_computation.32 | convolution fusion | flops 983056384 | bytes 5120512 | tf_op jit(solution)/shard_map/dot_general | solution.py:102
  38.5 1.7 %pad_maximum_fusion = f32[128,5050]{0,1:T(8,128)} fusion(f32[128,50]{0,1:T(8,128)S(1)} %fusion.18, f32[128,5000]{0,1:T(8,128)S(1)} %fusion.19), kind=kLoop, calls=%fused_computation.10 | loop fusion | flops 646400 | bytes 5171200 | tf_op jit(solution)/shard_map/concatenate | solution.py:46
  40.1 2.1 %copy.32 = f32[128,5050]{1,0:T(8,128)S(1)} copy(f32[128,5050]{0,1:T(8,128)} %pad_maximum_fusion) | data formatting | bytes 5171200 | tf_op jit(solution)/shard_map/concatenate | solution.py:46
  42.3 3.0 %copy.33 = f32[16,8,1,5050]{3,1,2,0:T(8,128)} copy(f32[16,8,1,5050]{3,0,1,2:T(8,128)S(1)} %bitcast.28) | data formatting | bytes 5171200 | tf_op jit(solution)/shard_map/transpose | solution.py:29
  45.3 7.6 %all-to-all-start.1 = ((f32[16,8,1,5050]{3,1,2,0:T(8,128)}), f32[16,8,1,5050]{3,1,2,0:T(8,128)S(1)}, u32[]{:S(2)}, u32[]{:S(2)}) async-start(f32[16,8,1,5050]{3,1,2,0:T(8,128)} %copy.33), calls=%async_computation.1 | async-start | bytes 5242880 | tf_op jit(solution)/shard_map/all_to_all | solution.py:34
  53.0 0.2 reduce_window_sum.11
  53.2 0.2 select_reduce_fusion
  53.4 1.0 scatter_custom_fusion
  54.4 1.2 gather_fusion.1
  55.8 0.8 gather_fusion
  56.5 0.9 copy.35
  57.4 32.1 %all-to-all-done.1 = f32[16,8,1,5050]{3,1,2,0:T(8,128)S(1)} async-done(((f32[16,8,1,5050]{3,1,2,0:T(8,128)}), f32[16,8,1,5050]{3,1,2,0:T(8,128)S(1)}, u32[]{:S(2)}, u32[]{:S(2)}) %all-to-all-start.1) | async-done | bytes 2585632 | tf_op jit(solution)/shard_map/all_to_all | solution.py:34
  89.5 16.4 %all-to-all-start.3 = ((f32[128,1,257]{2,1,0:T(1,128)}), f32[128,1,257]{2,1,0:T(1,128)S(1)}, u32[]{:S(2)}, u32[]{:S(2)}) async-start(f32[128,1,257]{2,1,0:T(1,128)} %copy.35), calls=%async_computation.3 | async-start | bytes 393216 | tf_op jit(solution)/shard_map/all_to_all | solution.py:63
  106.1 0.8 reduce_sum.52
  106.9 11.6 %all-to-all-done.3 = f32[128,1,257]{2,1,0:T(1,128)S(1)} async-done(((f32[128,1,257]{2,1,0:T(1,128)}), f32[128,1,257]{2,1,0:T(1,128)S(1)}, u32[]{:S(2)}, u32[]{:S(2)}) %all-to-all-start.3) | async-done | bytes 131616 | tf_op jit(solution)/shard_map/all_to_all | solution.py:63
  118.5 3.4 %all-to-all-start.2 = ((f32[8,1,5050]{2,1,0:T(1,128)}), f32[8,1,5050]{2,1,0:T(1,128)S(1)}, u32[]{:S(2)}, u32[]{:S(2)}) async-start(f32[8,1,5050]{2,1,0:T(1,128)} %reduce_sum.52), calls=%async_computation.2 | async-start | bytes 327680 | tf_op jit(solution)/shard_map/all_to_all | solution.py:41
  122.0 1.6 %scatter_custom_fusion.1 = f32[128,256]{1,0:T(8,128)} fusion(s32[128]{0:T(128)S(1)} %fusion.24, f32[128,257]{1,0:T(8,128)S(1)} %bitcast.29, f32[]{:T(128)} %constant.37.clone.1), kind=kCustom, calls=%fused_computation.18 | custom fusion | bytes 262148 | tf_op jit(solution)/shard_map/scatter | solution.py:138
  123.7 7.6 %all-to-all-done.2 = f32[8,1,5050]{2,1,0:T(1,128)S(1)} async-done(((f32[8,1,5050]{2,1,0:T(1,128)}), f32[8,1,5050]{2,1,0:T(1,128)S(1)}, u32[]{:S(2)}, u32[]{:S(2)}) %all-to-all-start.2) | async-done | bytes 161632 | tf_op jit(solution)/shard_map/all_to_all | solution.py:41
  131.4 0.6 slice.13
  132.1 0.7 copy.38
  (37 shorter events, 0.9 us)
Async XLA Ops:
  0.6 12.0 %copy-start = (f32[128,64]{0,1:T(8,128)S(1)}, f32[128,64]{0,1:T(8,128)}, u32[]{:S(2)}) copy-start(f32[128,64]{0,1:T(8,128)} %param.13) | copy-start | bytes 98308
  6.1 6.6 %copy-start.5 = (s32[128]{0:T(128)S(1)}, s32[128]{0:T(128)}, u32[]{:S(2)}) copy-start(s32[128]{0:T(128)} %param.14) | copy-start | bytes 1540
  6.1 6.6 %copy-start.7 = (s32[128]{0:T(128)S(1)}, s32[128]{0:T(128)}, u32[]{:S(2)}) copy-start(s32[128]{0:T(128)} %param.15) | copy-start | bytes 1540
  6.1 6.9 %copy-start.6 = (f32[128,64]{0,1:T(8,128)S(1)}, f32[128,64]{0,1:T(8,128)}, u32[]{:S(2)}) copy-start(f32[128,64]{0,1:T(8,128)} %param.12) | copy-start | bytes 98308
  6.1 7.2 %copy-start.2 = (f32[128,256]{1,0:T(8,128)S(1)}, f32[128,256]{1,0:T(8,128)}, u32[]{:S(2)}) copy-start(f32[128,256]{1,0:T(8,128)} %param.9) | copy-start | bytes 393220
  6.1 7.2 %copy-start.3 = (f32[128,256]{1,0:T(8,128)S(1)}, f32[128,256]{1,0:T(8,128)}, u32[]{:S(2)}) copy-start(f32[128,256]{1,0:T(8,128)} %param.10) | copy-start | bytes 393220
  6.1 7.2 %copy-start.4 = (s32[128]{0:T(128)S(1)}, s32[128]{0:T(128)}, u32[]{:S(2)}) copy-start(s32[128]{0:T(128)} %param.16) | copy-start | bytes 1540
  6.1 12.7 %all-to-all-start = ((bf16[128,100,256]{2,0,1:T(8,128)(2,1)}), bf16[128,100,256]{2,0,1:T(8,128)(2,1)}, u32[]{:S(2)}, u32[]{:S(2)}) async-start(bf16[128,100,256]{2,0,1:T(8,128)(2,1)} %bitcast.27), calls=%async_computation | async-start | bytes 13107200 | tf_op jit(solution)/shard_map/all_to_all | solution.py:13
  13.5 2.9 %copy-start.1 = (bf16[128,50,256]{2,0,1:T(8,128)(2,1)S(1)}, bf16[128,50,256]{2,0,1:T(8,128)(2,1)}, u32[]{:S(2)}) copy-start(bf16[128,50,256]{2,0,1:T(8,128)(2,1)} %param.11) | copy-start | bytes 9830404
  45.3 7.6 %copy-start.8 = (s32[128]{0:T(128)S(1)}, s32[128]{0:T(128)}, u32[]{:S(2)}) copy-start(s32[128]{0:T(128)} %param.17) | copy-start | bytes 1540
  45.3 44.2 %all-to-all-start.1 = ((f32[16,8,1,5050]{3,1,2,0:T(8,128)}), f32[16,8,1,5050]{3,1,2,0:T(8,128)S(1)}, u32[]{:S(2)}, u32[]{:S(2)}) async-start(f32[16,8,1,5050]{3,1,2,0:T(8,128)} %copy.33), calls=%async_computation.1 | async-start | bytes 5242880 | tf_op jit(solution)/shard_map/all_to_all | solution.py:34
  89.5 29.0 %all-to-all-start.3 = ((f32[128,1,257]{2,1,0:T(1,128)}), f32[128,1,257]{2,1,0:T(1,128)S(1)}, u32[]{:S(2)}, u32[]{:S(2)}) async-start(f32[128,1,257]{2,1,0:T(1,128)} %copy.35), calls=%async_computation.3 | async-start | bytes 393216 | tf_op jit(solution)/shard_map/all_to_all | solution.py:63
  118.5 12.7 %all-to-all-start.2 = ((f32[8,1,5050]{2,1,0:T(1,128)}), f32[8,1,5050]{2,1,0:T(1,128)S(1)}, u32[]{:S(2)}, u32[]{:S(2)}) async-start(f32[8,1,5050]{2,1,0:T(1,128)} %reduce_sum.52), calls=%async_computation.2 | async-start | bytes 327680 | tf_op jit(solution)/shard_map/all_to_all | solution.py:41
